TPU v7x, 32 devices: a whole 2x2x4 slice. The times are simulated.
32 devices in a mesh: grp: 8 (over z, y), mem: 4 (over x, core).
Axes of the slice: x: 2, y: 2, z: 4, core: 2. Of those that a mesh axis runs over, the one named last changes fastest.
Arguments:
- client_input: bfloat16 [8, 4, 128, 896], P('grp', 'mem'), may hold values from -6 to 6
- client_gain: float32 [4, 896], P('mem'), may hold values from 0.5 to 1.5
- w_query: bfloat16 [4, 896, 896], P('mem'), may hold values from -1.5 to 1.5
- w_keyval: bfloat16 [4, 896, 256], P('mem'), may hold values from -0.5 to 0.5
- w_out: bfloat16 [4, 896, 896], P('mem'), may hold values from -0.1875 to 0.1875
- server_gain: float32 [8, 896], P('grp'), may hold values from 0.5 to 1.5
- w_gate: bfloat16 [8, 896, 4864], P('grp', None, 'mem'), may hold values from -0.1875 to 0.1875
- w_up: bfloat16 [8, 896, 4864], P('grp', None, 'mem'), may hold values from -0.1875 to 0.1875
- w_down: bfloat16 [8, 4864, 896], P('grp', 'mem'), may hold values from -0.078125 to 0.078125
- out_grad: bfloat16 [8, 4, 128, 896], P('grp', 'mem'), may hold values from -6 to 6
- valid: int32 [8, 4], P('grp', 'mem'), may hold values from 64 to 128
Outputs:
- server_out: bfloat16 [8, 4, 128, 896], P('grp', 'mem')
- grad_query: bfloat16 [4, 896, 896], P('mem')
- grad_keyval: bfloat16 [4, 896, 256], P('mem')
- grad_out: bfloat16 [4, 896, 896], P('mem')
- grad_gate: bfloat16 [8, 896, 4864], P('grp', None, 'mem')
- grad_up: bfloat16 [8, 896, 4864], P('grp', None, 'mem')
- grad_down: bfloat16 [8, 4864, 896], P('grp', 'mem')
All inputs are finite; a program needn't handle non-finite values.
Results may differ from a plain program's by a relative error of at most 0.03.
Values may be sent and summed in bfloat16 or wider, within the bound.
A program may use at most 128 MiB of HBM per device.

v0:
```python
import functools

import jax
import jax.numpy as jnp
from jax import lax
from jax.experimental import pallas as pl
from jax.experimental.pallas import tpu as pltpu
from jax.sharding import PartitionSpec as P

KV_HEADS = 2
HEAD_DIM = 64


EPS = 1e-06
F32 = jnp.float32
BF16 = jnp.bfloat16
CONTRACT_LAST = (((1,), (1,)), ((), ()))
CONTRACT_FIRST = (((0,), (0,)), ((), ()))


def rms(h_float):
    return lax.rsqrt(jnp.mean(h_float * h_float, axis=-1, keepdims=True) + EPS)


def norm_back(h_float, inv_rms, gain_vec, upstream):
    scaled = upstream * gain_vec
    return inv_rms * scaled - h_float * inv_rms**3 * jnp.mean(
        scaled * h_float, axis=-1, keepdims=True
    )


def attention(queries, key_vals):
    length = queries.shape[0]
    half_cols = KV_HEADS * HEAD_DIM
    q_heads = queries.reshape(length, KV_HEADS, -1, HEAD_DIM)
    k_heads = key_vals[:, :half_cols].reshape(length, KV_HEADS, HEAD_DIM)
    v_heads = key_vals[:, half_cols:].reshape(length, KV_HEADS, HEAD_DIM)
    scores = jnp.einsum(
        "tgqd,sgd->gqts", q_heads, k_heads, preferred_element_type=F32
    ) * HEAD_DIM ** (-0.5)
    causal = jnp.arange(length)[:, None] >= jnp.arange(length)[None, :]
    scores = jnp.where(causal, scores, -1e30)
    highest = jnp.max(scores, axis=-1, keepdims=True)
    expo = jnp.exp(scores - highest)
    probs = (expo / jnp.sum(expo, axis=-1, keepdims=True)).astype(BF16)
    attended = jnp.einsum("gqts,sgd->tgqd", probs, v_heads, preferred_element_type=F32)
    return attended.astype(BF16).reshape(length, -1)


MESH = pl.DeviceIdType.MESH


class Gather:
    def __init__(self, axis, own, slots, sems, split=False):
        self.axis, self.own, self.slots, self.sems = axis, own, slots, sems
        self.taken = set()
        self.n = lax.axis_size(axis)
        self.pairs = self.n // 2
        me = lax.axis_index(axis)
        self.right = {axis: lax.rem(me + 2, self.n)}
        self.partner = {axis: me + 1 - 2 * lax.rem(me, 2)}
        self.split = split and self.pairs > 1
        self.cut_at = own.shape[0] // 2

    def source(self, step):
        return self.own if step == 0 else self.slots.at[2 * step]

    def ring_copy(self, step):
        ring_send, ring_recv = self.sems[0], self.sems[1]
        return pltpu.make_async_remote_copy(
            src_ref=self.source(step),
            dst_ref=self.slots.at[2 * step + 2],
            send_sem=ring_send.at[step],
            recv_sem=ring_recv.at[step],
            device_id=self.right,
            device_id_type=MESH,
        )

    def rest_copy(self):
        rows = pl.ds(self.cut_at, self.own.shape[0] - self.cut_at)
        last = 2 * self.pairs - 1
        return pltpu.make_async_remote_copy(
            src_ref=self.slots.at[last - 2, rows],
            dst_ref=self.slots.at[last, rows],
            send_sem=self.sems[0].at[self.pairs - 1],
            recv_sem=self.sems[1].at[self.pairs - 1],
            device_id=self.right,
            device_id_type=MESH,
        )

    def flip_copy(self, step):
        src, dst = self.source(step), self.slots.at[2 * step + 1]
        if self.split and step == self.pairs - 1:
            rows = pl.ds(0, self.cut_at)
            src, dst = self.slots.at[2 * step, rows], self.slots.at[2 * step + 1, rows]
        return pltpu.make_async_remote_copy(
            src_ref=src,
            dst_ref=dst,
            send_sem=self.sems[2].at[step],
            recv_sem=self.sems[3].at[step],
            device_id=self.partner,
            device_id_type=MESH,
        )

    def advance(self, step):
        if step > 0:
            self.ring_copy(step - 1).wait_recv()
        if step < self.pairs - 1:
            self.ring_copy(step).start()
        self.flip_copy(step).start()
        if self.split and step == self.pairs - 1:
            self.take(step - 1)
            self.rest_copy().start()

    def take(self, step):
        if step in self.taken:
            return
        self.taken.add(step)
        self.flip_copy(step).wait_recv()
        if self.split and step == self.pairs - 1:
            self.rest_copy().wait_recv()

    def finish(self):
        for step in range(self.pairs):
            if step < self.pairs - 1:
                self.ring_copy(step).wait_send()
            self.flip_copy(step).wait_send()
        if self.split:
            self.rest_copy().wait_send()


def gather_sems(n):
    pairs = n // 2
    return [
        pltpu.SemaphoreType.DMA((pairs,)),
        pltpu.SemaphoreType.DMA((pairs,)),
        pltpu.SemaphoreType.DMA((pairs,)),
        pltpu.SemaphoreType.DMA((pairs,)),
    ]


def greet(axes):
    barrier = pltpu.get_barrier_semaphore()
    count = 0
    for axis in axes:
        n = lax.axis_size(axis)
        me = lax.axis_index(axis)
        pl.semaphore_signal(
            barrier, 1, device_id={axis: me + 1 - 2 * lax.rem(me, 2)}, device_id_type=MESH
        )
        for k in range(1, n // 2):
            pl.semaphore_signal(
                barrier, 1, device_id={axis: lax.rem(me + 2 * k, n)}, device_id_type=MESH
            )
        count += n // 2
    pl.semaphore_wait(barrier, count)


def send(src, dst, sems, index, device):
    return pltpu.make_async_remote_copy(
        src_ref=src,
        dst_ref=dst,
        send_sem=sems[0].at[index],
        recv_sem=sems[1].at[index],
        device_id=device,
        device_id_type=MESH,
    )


def server_kernel(
    cut_own, cot_own, attended_own, normed_own, gain, gate_hbm, up_hbm, down_hbm,
    server_out, cut_grad, attended_far, normed_far, rows_normed_far, rows_cot_far,
    hidden_far, d_gate_far, d_up_far,
    attended_all, normed_all, rows_normed, rows_cot, hidden, d_gate, d_up, store_sem,
    gate_w, up_w, down_w, cut_slots, served, served_in, home_in, home_out, sums, give, give_in,
    passing, pass_in, load_sem, cut_sems, cot_sems, attended_sems, normed_sems, swap_sems, part_sems,
    home_sems, pass_sems,
):
    members, groups = lax.axis_size("mem"), lax.axis_size("grp")
    pairs, group_pairs = members // 2, groups // 2
    length, width = cut_own.shape
    half = length // 2
    me = lax.axis_index("mem")
    odd = lax.rem(me, 2)
    partner = {"mem": me + 1 - 2 * odd}
    loads = []
    for i, (far, near) in enumerate(((down_hbm, down_w), (gate_hbm, gate_w), (up_hbm, up_w))):
        loads.append(pltpu.make_async_copy(far, near, load_sem.at[i]))
        loads[-1].start()
    greet(("grp", "mem"))
    cut = Gather("mem", cut_own, cut_slots, cut_sems)
    cot = Gather("mem", cot_own, rows_cot, cot_sems)
    early = [
        Gather("grp", normed_own, normed_all, normed_sems, True),
        Gather("grp", attended_own, attended_all, attended_sems, True),
    ]
    cut.advance(0)
    cot.advance(0)
    for chain in early:
        chain.advance(0)
    cut_slots[0] = cut_own[...]
    rows_cot[0] = cot_own[...]
    normed_all[0] = normed_own[...]
    attended_all[0] = attended_own[...]
    sums[...] = cot_own[...].astype(F32)
    swaps = []
    pending = [(chain, step) for step in range(1, group_pairs) for chain in early]
    stores = []

    def keep_going():
        if pending:
            chain, step = pending.pop(0)
            chain.advance(step)

    def store(near, far):
        stores.append(pltpu.make_async_copy(near, far, store_sem.at[len(stores)]))
        stores[-1].start()

    for p in range(pairs):
        if p > 0:
            cut.advance(p)
            cot.advance(p)
        cut.take(p)
        cot.take(p)
        span = pl.ds(2 * p, 2)
        h_float = cut_slots[span].reshape(2 * length, width).astype(F32)
        inv_rms = rms(h_float)
        normed = (h_float * inv_rms * gain[...]).astype(BF16)
        rows_normed[span] = normed.reshape(2, length, width)
        if p == 0:
            for load in loads:
                load.wait()
        d_hidden = lax.dot_general(
            rows_cot[span].reshape(2 * length, width), down_w[...], CONTRACT_LAST,
            preferred_element_type=F32,
        )
        gate_act = lax.dot_general(normed, gate_w[...], CONTRACT_LAST, preferred_element_type=F32)
        up_act = lax.dot_general(normed, up_w[...], CONTRACT_LAST, preferred_element_type=F32)
        keep_going()
        sigma = jax.nn.sigmoid(gate_act)
        acted = gate_act * sigma
        hidden_now = (acted * up_act).astype(BF16)
        dg = (d_hidden * up_act * sigma * (1.0 + gate_act * (1.0 - sigma))).astype(BF16)
        du = (d_hidden * acted).astype(BF16)
        rows = pl.ds(2 * p * length, 2 * length)
        hidden[rows] = hidden_now
        d_gate[rows] = dg
        d_up[rows] = du
        d_normed = jnp.dot(dg, gate_w[...], preferred_element_type=F32)
        d_normed = d_normed + jnp.dot(du, up_w[...], preferred_element_type=F32)
        pushed = norm_back(h_float, inv_rms, gain[...], d_normed)
        sums[...] += pushed[:length] + pushed[length:]
        served[span] = (
            jnp.dot(hidden_now, down_w[...], preferred_element_type=F32)
            .astype(BF16)
            .reshape(2, length, width)
        )
        keep_going()
        for near, far in (
            (hidden, hidden_far), (d_gate, d_gate_far), (d_up, d_up_far)
        ):
            store(near.at[rows], far.at[rows])
        store(rows_normed.at[span], rows_normed_far.at[span])
        store(rows_cot.at[span], rows_cot_far.at[span])

    keep_rows = pl.ds(pl.multiple_of(odd * half, half), half)
    give_rows = pl.ds(pl.multiple_of((1 - odd) * half, half), half)
    give[...] = sums[give_rows].astype(BF16)
    handed = send(give, give_in, part_sems, 0, partner)
    handed.start()
    for p in range(pairs):
        swaps.append(send(served.at[2 * p + 1], served_in.at[p], swap_sems, p, partner))
        swaps[-1].start()
    handed.wait_recv()
    keep_going()
    total = sums[keep_rows] + give_in[...].astype(F32)
    passing[...] = total.astype(BF16)
    passes = []
    for k in range(1, pairs):
        passes.append(
            send(passing, pass_in.at[k - 1], pass_sems, k - 1, {"mem": lax.rem(me + 2 * k, members)})
        )
        passes[-1].start()
    homes = []
    for p in range(pairs):
        swaps[p].wait_recv()
        mine = served[2 * p].astype(F32) + served_in[p].astype(F32)
        if p == 0:
            result = cut_own[...].astype(F32) + mine
            sums[...] = result
        else:
            home_out[p - 1] = mine.astype(BF16)
            homes.append(
                send(
                    home_out.at[p - 1], home_in.at[p - 1], home_sems, p - 1,
                    {"mem": lax.rem(me + members - 2 * p, members)},
                )
            )
            homes[-1].start()
    for k in range(1, pairs):
        passes[k - 1].wait_recv()
        total = total + pass_in[k - 1].astype(F32)
    cut_grad[keep_rows] = (total / members).astype(BF16)
    back = send(cut_grad.at[keep_rows], cut_grad.at[keep_rows], part_sems, 1, partner)
    back.start()
    result = sums[...]
    for p in range(1, pairs):
        homes[p - 1].wait_recv()
        result = result + home_in[p - 1].astype(F32)
    server_out[...] = result.astype(BF16)
    while pending:
        keep_going()
    for chain, far in zip(early, (normed_far, attended_far)):
        for step in range(group_pairs):
            chain.take(step)
        store(chain.slots, far)
    for chain in early:
        chain.finish()
    for copy in stores:
        copy.wait()
    cut.finish()
    cot.finish()
    back.wait_recv()
    for copy in [handed, back] + swaps + passes + homes:
        copy.wait_send()


def server_call(cut, cot, attended, normed, gain, gate_t, up_t, down):
    members, groups = lax.axis_size("mem"), lax.axis_size("grp")
    pairs = members // 2
    length, width = cut.shape
    units = down.shape[0]
    half = length // 2
    rows = members * length
    shape = jax.ShapeDtypeStruct
    vmem = pl.BlockSpec(memory_space=pltpu.VMEM)
    far = pl.BlockSpec(memory_space=pl.ANY)
    others = max(pairs - 1, 1)
    two = lambda count: [pltpu.SemaphoreType.DMA((count,))] * 2
    return pl.pallas_call(
        server_kernel,
        out_shape=[
            shape((length, width), BF16),
            shape((length, width), BF16),
            shape((groups, length, width), BF16),
            shape((groups, length, width), BF16),
            shape((members, length, width), BF16),
            shape((members, length, width), BF16),
            shape((rows, units), BF16),
            shape((rows, units), BF16),
            shape((rows, units), BF16),
        ],
        in_specs=[vmem] * 5 + [far] * 3,
        out_specs=[vmem] * 2 + [far] * 7,
        scratch_shapes=[
            pltpu.VMEM((groups, length, width), BF16),
            pltpu.VMEM((groups, length, width), BF16),
            pltpu.VMEM((members, length, width), BF16),
            pltpu.VMEM((members, length, width), BF16),
            pltpu.VMEM((rows, units), BF16),
            pltpu.VMEM((rows, units), BF16),
            pltpu.VMEM((rows, units), BF16),
            pltpu.SemaphoreType.DMA((5 * pairs + 2,)),
            pltpu.VMEM((units, width), BF16),
            pltpu.VMEM((units, width), BF16),
            pltpu.VMEM((units, width), BF16),
            pltpu.VMEM((members, length, width), BF16),
            pltpu.VMEM((members, length, width), BF16),
            pltpu.VMEM((pairs, length, width), BF16),
            pltpu.VMEM((others, length, width), BF16),
            pltpu.VMEM((others, length, width), BF16),
            pltpu.VMEM((length, width), F32),
            pltpu.VMEM((half, width), BF16),
            pltpu.VMEM((half, width), BF16),
            pltpu.VMEM((half, width), BF16),
            pltpu.VMEM((others, half, width), BF16),
            pltpu.SemaphoreType.DMA((3,)),
            gather_sems(members),
            gather_sems(members),
            gather_sems(groups),
            gather_sems(groups),
            two(pairs),
            two(2),
            two(others),
            two(others),
        ],
        compiler_params=pltpu.CompilerParams(
            collective_id=0, has_side_effects=True, vmem_limit_bytes=60 * 2**20
        ),
        name="server",
    )(cut, cot, attended, normed, gain, gate_t, up_t, down)


def grads_kernel(
    d_own, cut_own, attended_far, normed_far, rows_normed_far, rows_cot_far,
    hidden_far, d_gate_far, d_up_far,
    grad_query, grad_keyval, grad_out, grad_gate_far, grad_up_far, grad_down_far,
    attended_all, normed_all, rows_normed, rows_cot, hidden, d_gate, d_up,
    grad_gate, grad_up, grad_down,
    d_slots, half_slots, half_in, acc, d_sems, half_sems, swap_sems, load_sem, store_sem,
):
    groups = lax.axis_size("grp")
    group_pairs = groups // 2
    length, width = cut_own.shape
    half = length // 2
    rows = rows_cot.shape[0] * length
    me = lax.axis_index("mem")
    odd = lax.rem(me, 2)
    half_own = cut_own.at[pl.ds(pl.multiple_of(odd * half, half), half)]
    partner = {"mem": me + 1 - 2 * odd}
    loads = []
    for i, (far, near) in enumerate((
        (hidden_far, hidden), (rows_cot_far, rows_cot), (d_gate_far, d_gate),
        (rows_normed_far, rows_normed), (d_up_far, d_up), (normed_far, normed_all),
        (attended_far, attended_all),
    )):
        loads.append(pltpu.make_async_copy(far, near, load_sem.at[i]))
        loads[-1].start()
    greet(("grp", "mem"))
    halves = Gather("grp", half_own, half_slots, half_sems, True)
    deltas = Gather("grp", d_own, d_slots, d_sems, True)
    chains = [halves, deltas]
    for chain in chains:
        chain.advance(0)
    half_slots[0] = half_own[...]
    d_slots[0] = d_own[...]
    pending = [(chain, step) for step in range(1, group_pairs) for chain in chains]

    def keep_going():
        if pending:
            chain, step = pending.pop(0)
            chain.advance(step)

    def weight_grad(left, right, out):
        out[...] = lax.dot_general(
            left[...], right[...].reshape(rows, width), CONTRACT_FIRST, preferred_element_type=F32
        ).astype(BF16)

    for load in loads:
        load.wait()
    stores = []
    for i, (left, right, near, far) in enumerate((
        (hidden, rows_cot, grad_down, grad_down_far),
        (d_gate, rows_normed, grad_gate, grad_gate_far),
        (d_up, rows_normed, grad_up, grad_up_far),
    )):
        weight_grad(left, right, near)
        stores.append(pltpu.make_async_copy(near, far, store_sem.at[i]))
        stores[-1].start()
        keep_going()
    while pending:
        keep_going()

    def grad_in(first, count):
        return lax.dot_general(
            normed_all[pl.ds(first, count)].reshape(count * length, width),
            d_slots[pl.ds(first, count)].reshape(count * length, d_slots.shape[2]),
            CONTRACT_FIRST,
            preferred_element_type=F32,
        )

    scale = 1.0 / groups
    ready = groups - 2
    for step in range(group_pairs - 1):
        deltas.take(step)
    acc[...] = grad_in(0, ready)
    for step in range(group_pairs):
        halves.take(step)
    swap = send(half_slots, half_in, swap_sems, 0, partner)
    swap.start()
    swap.wait_recv()
    mine = half_slots[...]
    other = half_in[...]
    top = jnp.where(odd == 0, mine, other)
    bottom = jnp.where(odd == 0, other, mine)
    top_att = attended_all[:, pl.ds(0, half), :].reshape(groups * half, width)
    low_att = attended_all[:, pl.ds(half, half), :].reshape(groups * half, width)
    out = lax.dot_general(
        top_att, top.reshape(groups * half, width), CONTRACT_FIRST, preferred_element_type=F32
    )
    out = out + lax.dot_general(
        low_att, bottom.reshape(groups * half, width), CONTRACT_FIRST, preferred_element_type=F32
    )
    grad_out[...] = (out * scale).astype(BF16)
    deltas.take(group_pairs - 1)
    split = grad_query.shape[1]
    result = (acc[...] + grad_in(ready, 2)) * scale
    grad_query[...] = result[:, :split].astype(BF16)
    grad_keyval[...] = result[:, split:].astype(BF16)
    for chain in chains:
        chain.finish()
    swap.wait_send()
    for copy in stores:
        copy.wait()


def grads_call(
    columns, d_own, cut_grad, attended_all, normed_all, rows_normed, rows_cot, hidden, d_gate, d_up
):
    groups = lax.axis_size("grp")
    width, (length, wide) = cut_grad.shape[1], d_own.shape
    half = length // 2
    units = hidden.shape[1]
    shape = jax.ShapeDtypeStruct
    vmem = pl.BlockSpec(memory_space=pltpu.VMEM)
    far = pl.BlockSpec(memory_space=pl.ANY)
    wide_operands = [attended_all, normed_all, rows_normed, rows_cot, hidden, d_gate, d_up]
    return pl.pallas_call(
        grads_kernel,
        out_shape=[
            shape((width, columns), BF16),
            shape((width, wide - columns), BF16),
            shape((width, width), BF16),
            shape((units, width), BF16),
            shape((units, width), BF16),
            shape((units, width), BF16),
        ],
        in_specs=[vmem] * 2 + [far] * 7,
        out_specs=[vmem] * 3 + [far] * 3,
        scratch_shapes=[pltpu.VMEM(a.shape, BF16) for a in wide_operands]
        + [pltpu.VMEM((units, width), BF16)] * 3
        + [
            pltpu.VMEM((groups, length, wide), BF16),
            pltpu.VMEM((groups, half, width), BF16),
            pltpu.VMEM((groups, half, width), BF16),
            pltpu.VMEM((width, wide), F32),
            gather_sems(groups),
            gather_sems(groups),
            [pltpu.SemaphoreType.DMA((1,))] * 2,
            pltpu.SemaphoreType.DMA((7,)),
            pltpu.SemaphoreType.DMA((3,)),
        ],
        compiler_params=pltpu.CompilerParams(
            collective_id=1, has_side_effects=True, vmem_limit_bytes=60 * 2**20
        ),
        name="grads",
    )(d_own, cut_grad, *wide_operands)


def hand_over_kernel(count, *refs):
    fars, outs, nears = refs[:count], refs[count : 2 * count], refs[2 * count : 3 * count]
    load_sem, store_sem = refs[3 * count :]
    pieces = []
    for far, out, near in zip(fars, outs, nears):
        rows = far.shape[0]
        parts = 2 if rows % 32 == 0 else 1
        for part in range(parts):
            span = pl.ds(part * (rows // parts), rows // parts)
            i = len(pieces)
            pieces.append((
                pltpu.make_async_copy(far.at[span], near.at[span], load_sem.at[i]),
                pltpu.make_async_copy(near.at[span], out.at[span], store_sem.at[i]),
            ))
    for load, _ in pieces:
        load.start()
    for load, store in pieces:
        load.wait()
        store.start()
    for _, store in pieces:
        store.wait()


def hand_over(arrays):
    far = pl.BlockSpec(memory_space=pl.ANY)
    count = len(arrays)
    return pl.pallas_call(
        functools.partial(hand_over_kernel, count),
        out_shape=[jax.ShapeDtypeStruct(a.shape, a.dtype) for a in arrays],
        in_specs=[far] * count,
        out_specs=[far] * count,
        scratch_shapes=[pltpu.VMEM(a.shape, a.dtype) for a in arrays]
        + [pltpu.SemaphoreType.DMA((2 * count,))] * 2,
        compiler_params=pltpu.CompilerParams(vmem_limit_bytes=60 * 2**20),
        name="results",
    )(*arrays)


def on_device(
    client_input,
    client_gain,
    w_query,
    w_keyval,
    w_out,
    server_gain,
    w_gate,
    w_up,
    w_down,
    out_grad,
    valid,
):
    tokens_in = client_input[0, 0]
    output_w = w_out[0]
    length, width = tokens_in.shape
    live = jnp.arange(length) < valid[0, 0]
    own_cot = jnp.where(live[:, None], out_grad[0, 0], jnp.zeros_like(out_grad[0, 0]))

    x_float = tokens_in.astype(F32)
    client_normed = (x_float * rms(x_float) * client_gain[0]).astype(BF16)
    queries = jnp.dot(client_normed, w_query[0], preferred_element_type=F32).astype(BF16)
    key_vals = jnp.dot(client_normed, w_keyval[0], preferred_element_type=F32).astype(BF16)
    attended, pull = jax.vjp(attention, queries, key_vals)
    mixed = jnp.dot(attended, output_w, preferred_element_type=F32)
    own_cut = (x_float + mixed).astype(BF16)

    (server_out, cut_grad, attended_all, normed_all, *rest) = server_call(
        own_cut, own_cot, attended, client_normed, server_gain, w_gate[0].T, w_up[0].T, w_down[0]
    )

    d_attended = lax.dot_general(
        cut_grad, output_w, CONTRACT_LAST, preferred_element_type=F32
    ).astype(BF16)
    d_queries, d_key_vals = pull(d_attended)
    grad_query, grad_keyval, grad_out, grad_gate, grad_up, grad_down = grads_call(
        queries.shape[1], jnp.concatenate([d_queries, d_key_vals], axis=1), cut_grad, attended_all, normed_all, *rest
    )
    (server_out, grad_query, grad_keyval, grad_out, grad_gate, grad_up, grad_down) = hand_over(
        [server_out, grad_query, grad_keyval, grad_out, grad_gate, grad_up, grad_down]
    )
    return (
        server_out[None, None],
        grad_query[None],
        grad_keyval[None],
        grad_out[None],
        grad_gate.T[None],
        grad_up.T[None],
        grad_down[None],
    )


def solution(mesh):
    in_specs = (
        P("grp", "mem", None, None),
        P("mem", None),
        P("mem", None, None),
        P("mem", None, None),
        P("mem", None, None),
        P("grp", None),
        P("grp", None, "mem"),
        P("grp", None, "mem"),
        P("grp", "mem", None),
        P("grp", "mem", None, None),
        P("grp", "mem"),
    )
    out_specs = (
        P("grp", "mem", None, None),
        P("mem", None, None),
        P("mem", None, None),
        P("mem", None, None),
        P("grp", None, "mem"),
        P("grp", None, "mem"),
        P("grp", "mem", None),
    )
    return jax.shard_map(
        on_device, mesh=mesh, in_specs=in_specs, out_specs=out_specs, check_vma=False
    )
```

profile of v0, /device:TPU:1, one launch (start us, length us, event | category | flops | bytes accessed | tf_op | source)
XLA Modules:
  0.0 116.7 jit_solution(2561992569581970874)
XLA Ops:
  0.6 0.0 copy-start
  0.6 0.0 copy-start.1
  1.4 1.1 fusion.34
  2.5 0.7 reduce
  3.3 1.4 %convolution_convert_fusion.3 = bf16[128,256]{1,0:T(8,128)(2,1)S(1)} fusion(bf16[1,896,256]{2,1,0:T(8,128)(2,1)} %param.14, bf16[1,1,128,896]{3,2,1,0:T(8,128)(2,1)} %param.11, f32[896]{0:T(1024)S(1)} %reduce, f32[128]{0:T(128)S(1)} %add_rsqrt_fusion), kind=kOutput, calls=%fused_computation.17 | convolution fusion | flops 59211776 | bytes 757760 | tf_op jit(solution)/shard_map/dot_general | solution.py:600
  4.7 0.1 copy.32
  4.8 0.1 copy.31
  5.0 1.7 %bitcast_select_fusion.1.cot_own = bf16[128,896]{1,0:T(8,128)(2,1)} fusion(bf16[1,1,128,896]{3,2,1,0:T(8,128)(2,1)} %param.20, pred[128]{0:T(512)(128)(4,1)S(1)} %iota_compare_fusion.2), kind=kLoop, calls=%fused_computation.51 | loop fusion | flops 114688 | bytes 458880 | tf_op jit(solution)/shard_map/jit(_where)/select_n | solution.py:595
  6.7 0.0 copy-done.1
  6.7 1.9 %fusion.9 = bf16[128,896]{1,0:T(8,128)(2,1)S(1)} fusion(bf16[1,896,896]{2,1,0:T(8,128)(2,1)} %param.13, bf16[1,1,128,896]{3,2,1,0:T(8,128)(2,1)S(1)} %copy-done.1, f32[896]{0:T(1024)S(1)} %reduce, f32[128]{0:T(128)S(1)} %add_rsqrt_fusion), kind=kOutput, calls=%fused_computation.12 | convolution fusion | flops 206094336 | bytes 2068480 | tf_op jit(solution)/shard_map/dot_general | solution.py:599
  8.6 0.2 copy.33
  8.8 0.0 copy-start.2
  8.8 0.8 fusion.36.normed_own
  9.6 0.3 fusion.31
  10.0 0.2 fusion.40
  10.1 0.0 copy-done.2
  10.1 0.6 multiply_divide_fusion
  10.8 0.2 divide_convert_fusion
  11.0 0.2 convolution_convert_fusion.1
  11.2 0.8 copy.35.attended_own
  12.0 0.0 copy-done
  12.0 1.2 fusion.15.cut_own
  13.2 45.2 %server.1 = (bf16[128,896]{1,0:T(8,128)(2,1)}, bf16[128,896]{1,0:T(8,128)(2,1)}, bf16[8,128,896]{2,1,0:T(8,128)(2,1)}, bf16[8,128,896]{2,1,0:T(8,128)(2,1)}, bf1...) custom-call(bf16[128,896]{1,0:T(8,128)(2,1)} %fusion.15.cut_own, ...), custom_call_target="tpu_custom_call" | custom-call | tf_op jit(solution)/shard_map/server/pallas_call | solution.py:340
  58.4 1.5 %fusion.12 = bf16[128,896]{1,0:T(8,128)(2,1)S(1)} fusion(bf16[128,896]{1,0:T(8,128)(2,1)} %get-tuple-element.30.cut_own, bf16[1,896,896]{2,1,0:T(8,128)(2,1)S(1)} %copy-done), kind=kOutput, calls=%fused_computation.13 | convolution fusion | flops 205635584 | bytes 2064384 | tf_op jit(solution)/shard_map/dot_general | solution.py:609
  60.0 0.2 copy.36
  60.2 0.5 fusion.18
  60.6 0.1 copy.38
  60.7 1.1 fusion.27
  61.9 0.0 copy-start.3
  61.9 0.4 fusion.30
  62.4 0.4 fusion.25
  62.8 0.0 copy-done.3
  62.8 0.3 fusion.19
  63.1 0.2 fusion.45
  63.3 0.2 copy.40
  63.5 0.1 copy.39
  63.7 0.7 pad_maximum_fusion.d_own
  64.4 43.9 %grads.1 = (bf16[896,896]{1,0:T(8,128)(2,1)}, bf16[896,256]{1,0:T(8,128)(2,1)}, bf16[896,896]{1,0:T(8,128)(2,1)}, bf16[1216,896]{1,0:T(8,128)(2,1)}, bf16[1216,8...) custom-call(bf16[128,1152]{1,0:T(8,128)(2,1)} %pad_maximum_fusion.d_own, bf16[128,896]{1,0:T(8,128)(2,1)} %get-tuple-element.30.cut_own, ...), custom_call_target="tpu_custom_call" | custom-call | tf_op jit(solution)/shard_map/grads/pallas_call | solution.py:508
  108.3 8.3 %results.1 = (bf16[128,896]{1,0:T(8,128)(2,1)}, bf16[896,896]{1,0:T(8,128)(2,1)}, bf16[896,256]{1,0:T(8,128)(2,1)}, bf16[896,896]{1,0:T(8,128)(2,1)}, bf16[1216,...) custom-call(bf16[128,896]{1,0:T(8,128)(2,1)} %get-tuple-element.29.refs_0_, ...), custom_call_target="tpu_custom_call" | custom-call | tf_op jit(solution)/shard_map/results/pallas_call | solution.py:566
  (8 shorter events, 0.1 us)
Async XLA Ops:
  0.6 11.4 %copy-start = (bf16[1,896,896]{2,1,0:T(8,128)(2,1)S(1)}, bf16[1,896,896]{2,1,0:T(8,128)(2,1)}, u32[]{:S(2)}) copy-start(bf16[1,896,896]{2,1,0:T(8,128)(2,1)} %param.15) | copy-start | bytes 4816900
  0.6 6.1 %copy-start.1 = (bf16[1,1,128,896]{3,2,1,0:T(8,128)(2,1)S(1)}, bf16[1,1,128,896]{3,2,1,0:T(8,128)(2,1)}, u32[]{:S(2)}) copy-start(bf16[1,1,128,896]{3,2,1,0:T(8,128)(2,1)} %param.11) | copy-start | bytes 688132
  8.8 1.3 %copy-start.2 = (bf16[128,896]{0,1:T(8,128)(2,1)}, bf16[128,896]{0,1:T(8,128)(2,1)S(1)}, u32[]{:S(2)}) copy-start(bf16[128,896]{0,1:T(8,128)(2,1)S(1)} %copy.33) | copy-start | bytes 688132
  61.9 0.9 copy-start.3
where the time goes:
time: 117 us
  Pallas kernels  97.4 us (83%)
  matrix products  8.66 us (7%)
  other arithmetic  6.99 us (6%)
  local copies, waits for them, and re-layouts  1.86 us (2%)
  between operations  1.8 us (2%)
    pallas_call x1, Pallas kernels, server_call(): pl.pallas_call(server_kernel, out_shape=[shape((length, width), BF16), sh...  45.2 us
    pallas_call x1, Pallas kernels, grads_call(): pl.pallas_call(grads_kernel, out_shape=[shape((width, columns), BF16), sh...  43.9 us
    pallas_call x1, Pallas kernels, hand_over(): pl.pallas_call(functools.partial(hand_over_kernel, count), out_shape=[jax...  8.26 us

commit v1 on v0

v1 whole, which is shorter than its diff:
```python
import jax
import jax.numpy as jnp
from jax import lax
from jax.experimental import pallas as pl
from jax.experimental.pallas import tpu as pltpu
from jax.sharding import PartitionSpec as P

KV_HEADS = 2
HEAD_DIM = 64


EPS = 1e-06
F32 = jnp.float32
BF16 = jnp.bfloat16
CONTRACT_LAST = (((1,), (1,)), ((), ()))
CONTRACT_FIRST = (((0,), (0,)), ((), ()))
FIRST_WITH_LAST = (((0,), (1,)), ((), ()))
MESH = pl.DeviceIdType.MESH
SCALE = HEAD_DIM ** (-0.5)


def rms(h_float):
    return lax.rsqrt(jnp.mean(h_float * h_float, axis=-1, keepdims=True) + EPS)


def norm_back(h_float, inv_rms, gain_vec, upstream):
    scaled = upstream * gain_vec
    return inv_rms * scaled - h_float * inv_rms**3 * jnp.mean(
        scaled * h_float, axis=-1, keepdims=True
    )


def dot(left, right, dims=(((1,), (0,)), ((), ()))):
    return lax.dot_general(left, right, dims, preferred_element_type=F32)


class Gather:
    def __init__(self, axis, slot, rows, sems, split=False):
        self.axis, self.slot, self.rows, self.sems = axis, slot, rows, sems
        self.taken = set()
        self.n = lax.axis_size(axis)
        self.pairs = self.n // 2
        me = lax.axis_index(axis)
        self.right = {axis: lax.rem(me + 2, self.n)}
        self.partner = {axis: me + 1 - 2 * lax.rem(me, 2)}
        self.split = split and self.pairs > 1
        self.cut_at = rows // 2

    def send(self, src, dst, first, index, device):
        return pltpu.make_async_remote_copy(
            src_ref=src,
            dst_ref=dst,
            send_sem=self.sems[first].at[index],
            recv_sem=self.sems[first + 1].at[index],
            device_id=device,
            device_id_type=MESH,
        )

    def ring_copy(self, step):
        src, dst = self.slot(2 * step, 0, self.rows), self.slot(2 * step + 2, 0, self.rows)
        return self.send(src, dst, 0, step, self.right)

    def rest_copy(self):
        last, low, count = 2 * self.pairs - 1, self.cut_at, self.rows - self.cut_at
        src, dst = self.slot(last - 2, low, count), self.slot(last, low, count)
        return self.send(src, dst, 0, self.pairs - 1, self.right)

    def flip_copy(self, step):
        rows = self.cut_at if self.split and step == self.pairs - 1 else self.rows
        src, dst = self.slot(2 * step, 0, rows), self.slot(2 * step + 1, 0, rows)
        return self.send(src, dst, 2, step, self.partner)

    def advance(self, step):
        if step > 0:
            self.ring_copy(step - 1).wait_recv()
        if step < self.pairs - 1:
            self.ring_copy(step).start()
        self.flip_copy(step).start()
        if self.split and step == self.pairs - 1:
            self.take(step - 1)
            self.rest_copy().start()

    def take(self, step):
        if step in self.taken:
            return
        self.taken.add(step)
        self.flip_copy(step).wait_recv()
        if self.split and step == self.pairs - 1:
            self.rest_copy().wait_recv()

    def finish(self):
        for step in range(self.pairs):
            if step < self.pairs - 1:
                self.ring_copy(step).wait_send()
            self.flip_copy(step).wait_send()
        if self.split:
            self.rest_copy().wait_send()


def gather_sems(n):
    return [pltpu.SemaphoreType.DMA((n // 2,))] * 4


def greet(axes):
    barrier = pltpu.get_barrier_semaphore()
    count = 0
    for axis in axes:
        n = lax.axis_size(axis)
        me = lax.axis_index(axis)
        pl.semaphore_signal(
            barrier, 1, device_id={axis: me + 1 - 2 * lax.rem(me, 2)}, device_id_type=MESH
        )
        for k in range(1, n // 2):
            pl.semaphore_signal(
                barrier, 1, device_id={axis: lax.rem(me + 2 * k, n)}, device_id_type=MESH
            )
        count += n // 2
    pl.semaphore_wait(barrier, count)


def send(src, dst, sems, index, device):
    return pltpu.make_async_remote_copy(
        src_ref=src,
        dst_ref=dst,
        send_sem=sems[0].at[index],
        recv_sem=sems[1].at[index],
        device_id=device,
        device_id_type=MESH,
    )


def step_kernel(
    x_own, og_own, valid, c_gain, s_gain, wq_far, wkv_far, wo_far, gate_far, up_far, down_far,
    server_out_far, g_gate_far, g_up_far, g_down_far, normed_far, att_far, dqkv_far, cg_far,
    wq, wkv, wo, gate_w, up_w, down_w,
    normed_all, q_all, kv_all, p_all, att_all, dqkv_all, cg_all,
    cut_slots, rows_cot, rows_normed, hidden, d_gate, d_up, g_gate, g_up, g_down,
    served, served_in, home_in, home_out, sums, result, give, give_in, passing, pass_in,
    load_sem, store_sem, early_sems, late_sems, cut_sems, cot_sems,
    swap_sems, part_sems, home_sems, pass_sems, half_sems,
):
    members, groups = lax.axis_size("mem"), lax.axis_size("grp")
    pairs, group_pairs = members // 2, groups // 2
    length, width = x_own.shape
    half = length // 2
    me = lax.axis_index("mem")
    odd = lax.rem(me, 2)
    partner = {"mem": me + 1 - 2 * odd}
    q_cols = wq.shape[1]
    per_kv = q_cols // HEAD_DIM // KV_HEADS
    kv_rows = KV_HEADS * HEAD_DIM

    loads = {}
    for i, (name, far, near) in enumerate((
        ("wq", wq_far, wq), ("wkv", wkv_far, wkv), ("wo", wo_far, wo),
        ("down", down_far, down_w), ("gate", gate_far, gate_w), ("up", up_far, up_w),
    )):
        loads[name] = pltpu.make_async_copy(far, near, load_sem.at[i])
        loads[name].start()
    stores = []

    def store(near, far):
        stores.append(pltpu.make_async_copy(near, far, store_sem.at[len(stores)]))
        stores[-1].start()

    keep_at = pl.multiple_of(odd * half, half)
    give_at = pl.multiple_of((1 - odd) * half, half)

    def half_slot(index, low, count):
        return cg_all.at[index, pl.ds(pl.multiple_of(keep_at + low, 8), count)]

    def whole(ref):
        return lambda index, low, count: ref.at[index, pl.ds(low, count)]

    cut = Gather("mem", whole(cut_slots), length, cut_sems)
    cot = Gather("mem", whole(rows_cot), length, cot_sems)
    early = Gather("grp", whole(normed_all), length, early_sems, True)
    late = Gather("grp", half_slot, half, late_sems, True)

    live = lax.broadcasted_iota(jnp.int32, (length, width), 0) < valid[0, 0]
    own_cot = jnp.where(live, og_own[...].astype(F32), 0.0)
    rows_cot[0] = own_cot.astype(BF16)
    sums[...] = own_cot
    x_float = x_own[...].astype(F32)
    normed_all[0] = (x_float * rms(x_float) * c_gain[...]).astype(BF16)
    greet(("grp", "mem"))
    cot.advance(0)
    early.advance(0)

    key_at = lax.broadcasted_iota(jnp.int32, (length, length), 0)
    query_at = lax.broadcasted_iota(jnp.int32, (length, length), 1)
    bias = jnp.where(key_at <= query_at, 0.0, -1e30).astype(F32)
    bias = jnp.concatenate([bias] * per_kv, axis=1)

    def side_by_side(rows, kv):
        first = kv * per_kv * HEAD_DIM
        return jnp.concatenate(
            [rows[first + i * HEAD_DIM : first + (i + 1) * HEAD_DIM] for i in range(per_kv)], axis=1
        )

    def stacked(columns):
        return jnp.concatenate(
            [columns[:, i * length : (i + 1) * length] for i in range(per_kv)], axis=0
        )

    def forward(first, count):
        normed = normed_all[pl.ds(first, count)].reshape(count * length, width)
        queries = (dot(normed, wq[...]) * SCALE).astype(BF16).T
        key_vals = dot(normed, wkv[...]).astype(BF16).T
        for i in range(count):
            slot, span = first + i, slice(i * length, (i + 1) * length)
            kv_all[slot] = key_vals[:, span]
            for kv in range(KV_HEADS):
                keys = key_vals[kv * HEAD_DIM : (kv + 1) * HEAD_DIM, span]
                vals = key_vals[kv_rows + kv * HEAD_DIM : kv_rows + (kv + 1) * HEAD_DIM, span]
                q_cat = side_by_side(queries[:, span], kv)
                q_all[slot, kv] = q_cat
                scores = dot(keys, q_cat, CONTRACT_FIRST) + bias
                expo = jnp.exp(scores - jnp.max(scores, axis=0, keepdims=True))
                probs = (expo * (1.0 / jnp.sum(expo, axis=0, keepdims=True))).astype(BF16)
                p_all[slot, kv] = probs
                att_all[
                    pl.ds(kv * per_kv * HEAD_DIM, per_kv * HEAD_DIM), pl.ds(slot * length, length)
                ] = stacked(dot(vals, probs).astype(BF16))

    def backward(first, count):
        upstream = cg_all[pl.ds(first, count)].reshape(count * length, width)
        d_att = dot(wo[...], upstream, CONTRACT_LAST).astype(BF16)
        for i in range(count):
            slot, span = first + i, slice(i * length, (i + 1) * length)
            columns = pl.ds(slot * length, length)
            for kv in range(KV_HEADS):
                keys = kv_all[slot, pl.ds(kv * HEAD_DIM, HEAD_DIM)]
                vals = kv_all[slot, pl.ds(kv_rows + kv * HEAD_DIM, HEAD_DIM)]
                d_cat = side_by_side(d_att[:, span], kv)
                probs = p_all[slot, kv]
                weighed = dot(vals, d_cat, CONTRACT_FIRST)
                p_float = probs.astype(F32)
                weighed = weighed * p_float
                d_scores = weighed - p_float * jnp.sum(weighed, axis=0, keepdims=True)
                d_scores = d_scores.astype(BF16)
                d_q = (dot(keys, d_scores) * SCALE).astype(BF16)
                dqkv_all[pl.ds(kv * per_kv * HEAD_DIM, per_kv * HEAD_DIM), columns] = stacked(d_q)
                dqkv_all[pl.ds(q_cols + kv * HEAD_DIM, HEAD_DIM), columns] = dot(
                    q_all[slot, kv], d_scores, CONTRACT_LAST
                ).astype(BF16)
                dqkv_all[pl.ds(q_cols + kv_rows + kv * HEAD_DIM, HEAD_DIM), columns] = dot(
                    d_cat, probs, CONTRACT_LAST
                ).astype(BF16)

    loads["wq"].wait()
    loads["wkv"].wait()
    forward(0, 1)
    loads["wo"].wait()
    mixed = dot(att_all[:, pl.ds(0, length)], wo[...], CONTRACT_FIRST)
    cut_slots[0] = (x_own[...].astype(F32) + mixed).astype(BF16)
    cut.advance(0)

    early_steps = list(range(1, group_pairs))
    ready = [1, 1]

    def keep_going():
        if early_steps:
            step = early_steps.pop(0)
            early.advance(step)
            ready[1] = 2 * step

    def recompute(limit):
        while ready[0] < min(limit, groups):
            first = ready[0]
            count = 1 if first % 2 else 2
            early.take((first + count - 1) // 2)
            forward(first, count)
            ready[0] += count

    for p in range(pairs):
        if p > 0:
            cut.advance(p)
            cot.advance(p)
        cut.take(p)
        cot.take(p)
        span = pl.ds(2 * p, 2)
        h_float = cut_slots[span].reshape(2 * length, width).astype(F32)
        inv_rms = rms(h_float)
        normed = (h_float * inv_rms * s_gain[...]).astype(BF16)
        rows_normed[span] = normed.reshape(2, length, width)
        if p == 0:
            for name in ("down", "gate", "up"):
                loads[name].wait()
        d_hidden = dot(rows_cot[span].reshape(2 * length, width), down_w[...], CONTRACT_LAST)
        gate_act = dot(normed, gate_w[...], CONTRACT_LAST)
        up_act = dot(normed, up_w[...], CONTRACT_LAST)
        if p > 0:
            keep_going()
        sigma = jax.nn.sigmoid(gate_act)
        acted = gate_act * sigma
        hidden_now = (acted * up_act).astype(BF16)
        dg = (d_hidden * up_act * sigma * (1.0 + gate_act * (1.0 - sigma))).astype(BF16)
        du = (d_hidden * acted).astype(BF16)
        rows = pl.ds(2 * p * length, 2 * length)
        hidden[rows] = hidden_now
        d_gate[rows] = dg
        d_up[rows] = du
        d_normed = dot(dg, gate_w[...]) + dot(du, up_w[...])
        pushed = norm_back(h_float, inv_rms, s_gain[...], d_normed)
        sums[...] += pushed[:length] + pushed[length:]
        served[span] = dot(hidden_now, down_w[...]).astype(BF16).reshape(2, length, width)
        if p == 0:
            keep_going()
            recompute(2)

    give[...] = sums[pl.ds(give_at, half)].astype(BF16)
    handed = send(give, give_in, part_sems, 0, partner)
    handed.start()
    swaps = []
    for p in range(pairs):
        swaps.append(send(served.at[2 * p + 1], served_in.at[p], swap_sems, p, partner))
        swaps[-1].start()
    handed.wait_recv()
    total = sums[pl.ds(keep_at, half)] + give_in[...].astype(F32)
    passing[...] = total.astype(BF16)
    passes = []
    for k in range(1, pairs):
        passes.append(
            send(passing, pass_in.at[k - 1], pass_sems, k - 1, {"mem": lax.rem(me + 2 * k, members)})
        )
        passes[-1].start()
    keep_going()
    recompute(4)
    homes = []
    for p in range(pairs):
        swaps[p].wait_recv()
        mine = served[2 * p].astype(F32) + served_in[p].astype(F32)
        if p == 0:
            result[...] = cut_slots[0].astype(F32) + mine
        else:
            home_out[p - 1] = mine.astype(BF16)
            homes.append(
                send(
                    home_out.at[p - 1], home_in.at[p - 1], home_sems, p - 1,
                    {"mem": lax.rem(me + members - 2 * p, members)},
                )
            )
            homes[-1].start()
    for k in range(1, pairs):
        passes[k - 1].wait_recv()
        total = total + pass_in[k - 1].astype(F32)
    cg_all[0, pl.ds(keep_at, half)] = (total / members).astype(BF16)

    exchanged = {}

    def exchange(slot):
        ref = half_slot(slot, 0, half)
        exchanged[slot] = send(ref, ref, half_sems, slot, partner)
        exchanged[slot].start()

    late.advance(0)
    exchange(0)
    keep_going()

    def weight_grad(left, right, near, far):
        rows = right.shape[0] * length
        near[...] = dot(left[...], right[...].reshape(rows, width), CONTRACT_FIRST).astype(BF16)
        store(near, far)

    weight_grads = [
        (hidden, rows_cot, g_down, g_down_far),
        (d_gate, rows_normed, g_gate, g_gate_far),
        (d_up, rows_normed, g_up, g_up_far),
    ]

    def more():
        if weight_grads:
            weight_grad(*weight_grads.pop(0))

    recompute(6)
    more()
    while early_steps:
        keep_going()
    for step in range(1, group_pairs):
        late.advance(step)
        exchange(2 * step)
        late.take(step - 1)
        exchange(2 * step - 1)
        recompute(groups if step > 1 else 6)
        more()
        if step == 1:
            for p in range(1, pairs):
                homes[p - 1].wait_recv()
                result[...] += home_in[p - 1].astype(F32)
            served[0] = result[...].astype(BF16)
            store(served.at[0], server_out_far)
        if step > 1:
            for slot in (2 * step - 4, 2 * step - 3):
                exchanged[slot].wait_recv()
            backward(2 * step - 4, 2)
    while early_steps:
        keep_going()
    recompute(groups)
    while weight_grads:
        more()
    store(normed_all, normed_far)
    store(att_all, att_far)
    late.take(group_pairs - 1)
    exchange(groups - 1)
    for first in range(max(groups - 4, 0), groups, 2):
        for slot in (first, first + 1):
            exchanged[slot].wait_recv()
        backward(first, 2)
    store(cg_all, cg_far)
    store(dqkv_all, dqkv_far)
    early.finish()
    late.finish()
    cut.finish()
    cot.finish()
    for copy in [handed] + swaps + passes + homes + list(exchanged.values()):
        copy.wait_send()
    for copy in stores:
        copy.wait()


def step_call(x, og, valid, c_gain, s_gain, wq, wkv, wo, gate_t, up_t, down):
    members, groups = lax.axis_size("mem"), lax.axis_size("grp")
    pairs = members // 2
    length, width = x.shape
    units = down.shape[0]
    q_cols, kv_cols = wq.shape[1], wkv.shape[1]
    per_kv = q_cols // HEAD_DIM // KV_HEADS
    half = length // 2
    rows = members * length
    tokens = groups * length
    shape = jax.ShapeDtypeStruct
    near = pl.BlockSpec(memory_space=pltpu.VMEM)
    far = pl.BlockSpec(memory_space=pl.ANY)
    others = max(pairs - 1, 1)
    two = lambda count: [pltpu.SemaphoreType.DMA((count,))] * 2
    vmem = lambda *dims: pltpu.VMEM(dims, BF16)
    return pl.pallas_call(
        step_kernel,
        out_shape=[
            shape((length, width), BF16),
            shape((units, width), BF16),
            shape((units, width), BF16),
            shape((units, width), BF16),
            shape((groups, length, width), BF16),
            shape((q_cols, tokens), BF16),
            shape((q_cols + kv_cols, tokens), BF16),
            shape((groups, length, width), BF16),
        ],
        in_specs=[near] * 2 + [pl.BlockSpec(memory_space=pltpu.SMEM)] + [near] * 2 + [far] * 6,
        out_specs=[far] * 8,
        scratch_shapes=[
            vmem(*wq.shape), vmem(*wkv.shape), vmem(*wo.shape),
            vmem(units, width), vmem(units, width), vmem(units, width),
            vmem(groups, length, width),
            vmem(groups, KV_HEADS, HEAD_DIM, per_kv * length),
            vmem(groups, kv_cols, length),
            vmem(groups, KV_HEADS, length, per_kv * length),
            vmem(q_cols, tokens),
            vmem(q_cols + kv_cols, tokens),
            vmem(groups, length, width),
            vmem(members, length, width), vmem(members, length, width), vmem(members, length, width),
            vmem(rows, units), vmem(rows, units), vmem(rows, units),
            vmem(units, width), vmem(units, width), vmem(units, width),
            vmem(members, length, width),
            vmem(pairs, length, width),
            vmem(others, length, width),
            vmem(others, length, width),
            pltpu.VMEM((length, width), F32),
            pltpu.VMEM((length, width), F32),
            vmem(half, width), vmem(half, width), vmem(half, width),
            vmem(others, half, width),
            pltpu.SemaphoreType.DMA((6,)),
            pltpu.SemaphoreType.DMA((8,)),
            gather_sems(groups), gather_sems(groups), gather_sems(members), gather_sems(members),
            two(pairs), two(1), two(others), two(others), two(groups),
        ],
        compiler_params=pltpu.CompilerParams(
            collective_id=0, has_side_effects=True, vmem_limit_bytes=67043328
        ),
        name="step",
    )(x, og, valid, c_gain, s_gain, wq, wkv, wo, gate_t, up_t, down)


def grads_kernel(
    groups, server_far, gate_far, up_far, down_far, normed_far, att_far, dqkv_far, cg_far,
    server_out, g_query_out, g_keyval_out, g_out_out, g_gate_out, g_up_out, g_down_out,
    server, gate, up, down, normed, att, dqkv, cg, g_query, g_keyval, g_out, load_sem, store_sem,
):
    tokens = att.shape[1]
    width = normed.shape[2]
    columns = g_query.shape[1]
    loads = {}
    for i, (name, source, near) in enumerate((
        ("att", att_far, att), ("cg", cg_far, cg), ("normed", normed_far, normed),
        ("dqkv", dqkv_far, dqkv), ("down", down_far, down), ("gate", gate_far, gate),
        ("up", up_far, up), ("server", server_far, server),
    )):
        loads[name] = pltpu.make_async_copy(source, near, load_sem.at[i])
        loads[name].start()
    stores = []

    def store(near, out):
        stores.append(pltpu.make_async_copy(near, out, store_sem.at[len(stores)]))
        stores[-1].start()

    scale = 1.0 / groups
    loads["att"].wait()
    loads["cg"].wait()
    g_out[...] = (dot(att[...], cg[...].reshape(tokens, width)) * scale).astype(BF16)
    store(g_out, g_out_out)
    loads["normed"].wait()
    loads["dqkv"].wait()
    for name, near, out in (("down", down, g_down_out), ("gate", gate, g_gate_out)):
        loads[name].wait()
        store(near, out)
    grads = dot(normed[...].reshape(tokens, width), dqkv[...], FIRST_WITH_LAST) * scale
    g_query[...] = grads[:, :columns].astype(BF16)
    store(g_query, g_query_out)
    g_keyval[...] = grads[:, columns:].astype(BF16)
    store(g_keyval, g_keyval_out)
    for name, near, out in (("up", up, g_up_out), ("server", server, server_out)):
        loads[name].wait()
        store(near, out)
    for copy in stores:
        copy.wait()


def grads_call(columns, *arrays):
    server, gate, up, down, normed, att, dqkv, cg = arrays
    groups, _, width = normed.shape
    wide = dqkv.shape[0]
    far = pl.BlockSpec(memory_space=pl.ANY)
    outs = [
        server.shape, (width, columns), (width, wide - columns), (att.shape[0], width),
        gate.shape, up.shape, down.shape,
    ]
    return pl.pallas_call(
        lambda *refs: grads_kernel(groups, *refs),
        out_shape=[jax.ShapeDtypeStruct(o, BF16) for o in outs],
        in_specs=[far] * len(arrays),
        out_specs=[far] * len(outs),
        scratch_shapes=[pltpu.VMEM(a.shape, BF16) for a in arrays]
        + [pltpu.VMEM(o, BF16) for o in outs[1:4]]
        + [pltpu.SemaphoreType.DMA((len(arrays),)), pltpu.SemaphoreType.DMA((len(outs),))],
        compiler_params=pltpu.CompilerParams(vmem_limit_bytes=67043328),
        name="grads",
    )(*arrays)


def on_device(
    client_input,
    client_gain,
    w_query,
    w_keyval,
    w_out,
    server_gain,
    w_gate,
    w_up,
    w_down,
    out_grad,
    valid,
):
    server, gate, up, down, normed, att, dqkv, cg = step_call(
        client_input[0, 0], out_grad[0, 0], valid, client_gain, server_gain,
        w_query[0], w_keyval[0], w_out[0], w_gate[0].T, w_up[0].T, w_down[0],
    )
    (server_out, grad_query, grad_keyval, grad_out, grad_gate, grad_up, grad_down) = grads_call(
        w_query.shape[2], server, gate, up, down, normed, att, dqkv, cg
    )
    return (
        server_out[None, None],
        grad_query[None],
        grad_keyval[None],
        grad_out[None],
        grad_gate.T[None],
        grad_up.T[None],
        grad_down[None],
    )


def solution(mesh):
    in_specs = (
        P("grp", "mem", None, None),
        P("mem", None),
        P("mem", None, None),
        P("mem", None, None),
        P("mem", None, None),
        P("grp", None),
        P("grp", None, "mem"),
        P("grp", None, "mem"),
        P("grp", "mem", None),
        P("grp", "mem", None, None),
        P("grp", "mem"),
    )
    out_specs = (
        P("grp", "mem", None, None),
        P("mem", None, None),
        P("mem", None, None),
        P("mem", None, None),
        P("grp", None, "mem"),
        P("grp", None, "mem"),
        P("grp", "mem", None),
    )
    return jax.shard_map(
        on_device, mesh=mesh, in_specs=in_specs, out_specs=out_specs, check_vma=False
    )
```

time: 117 us -> 70.1 us (0.60)
  the two profiles are of different devices: /device:TPU:1 before, /device:TPU:0 now
where the time goes in v1:
time: 70.1 us; the launch traced here: 69.9 us
  Pallas kernels  68.5 us (98%)
  between operations  1.47 us (2%)
    pallas_call x1, Pallas kernels, step_call(): pl.pallas_call(step_kernel, out_shape=[shape((length, width), BF16), shap...  59.2 us
    pallas_call x1, Pallas kernels, grads_call(): pl.pallas_call(lambda *refs: grads_kernel(groups, *refs), out_shape=[jax....  9.27 us

profile of v1, /device:TPU:0, one launch (start us, length us, event | category | flops | bytes accessed | tf_op | source)
XLA Modules:
  0.0 69.9 jit_solution(7565853611477530935)
XLA Ops:
  1.3 59.2 %step.1 = (bf16[128,896]{1,0:T(8,128)(2,1)}, bf16[1216,896]{1,0:T(8,128)(2,1)}, bf16[1216,896]{1,0:T(8,128)(2,1)}, bf16[1216,896]{1,0:T(8,128)(2,1)}, bf16[8,128...) custom-call(bf16[128,896]{1,0:T(8,128)(2,1)} %bitcast.29, ...), custom_call_target="tpu_custom_call" | custom-call | tf_op jit(solution)/shard_map/step/pallas_call | solution.py:438
  60.5 9.3 %grads.1 = (bf16[128,896]{1,0:T(8,128)(2,1)}, bf16[896,896]{1,0:T(8,128)(2,1)}, bf16[896,256]{1,0:T(8,128)(2,1)}, bf16[896,896]{1,0:T(8,128)(2,1)}, bf16[1216,89...) custom-call(bf16[128,896]{1,0:T(8,128)(2,1)} %get-tuple-element.22.refs_0_, ...), custom_call_target="tpu_custom_call" | custom-call | tf_op jit(solution)/shard_map/grads/pallas_call | solution.py:538

commit v2 on v1

--- a/solution.py
+++ b/solution.py
@@ -1,3 +1,6 @@
+import functools
+import math
+
 import jax
 import jax.numpy as jnp
 from jax import lax
@@ -10,6 +13,7 @@
 
 
 EPS = 1e-06
+VMEM_MOST = 67043328
 F32 = jnp.float32
 BF16 = jnp.bfloat16
 CONTRACT_LAST = (((1,), (1,)), ((), ()))
@@ -70,15 +74,19 @@
         src, dst = self.slot(2 * step, 0, rows), self.slot(2 * step + 1, 0, rows)
         return self.send(src, dst, 2, step, self.partner)
 
-    def advance(self, step):
+    def advance(self, step, ring=True):
         if step > 0:
             self.ring_copy(step - 1).wait_recv()
-        if step < self.pairs - 1:
-            self.ring_copy(step).start()
+        if ring:
+            self.pass_on(step)
         self.flip_copy(step).start()
         if self.split and step == self.pairs - 1:
             self.take(step - 1)
             self.rest_copy().start()
+
+    def pass_on(self, step):
+        if step < self.pairs - 1:
+            self.ring_copy(step).start()
 
     def take(self, step):
         if step in self.taken:
@@ -115,7 +123,7 @@
                 barrier, 1, device_id={axis: lax.rem(me + 2 * k, n)}, device_id_type=MESH
             )
         count += n // 2
-    pl.semaphore_wait(barrier, count)
+    return lambda: pl.semaphore_wait(barrier, count)
 
 
 def send(src, dst, sems, index, device):
@@ -130,13 +138,13 @@
 
 
 def step_kernel(
-    x_own, og_own, valid, c_gain, s_gain, wq_far, wkv_far, wo_far, gate_far, up_far, down_far,
-    server_out_far, g_gate_far, g_up_far, g_down_far, normed_far, att_far, dqkv_far, cg_far,
-    wq, wkv, wo, gate_w, up_w, down_w,
-    normed_all, q_all, kv_all, p_all, att_all, dqkv_all, cg_all,
-    cut_slots, rows_cot, rows_normed, hidden, d_gate, d_up, g_gate, g_up, g_down,
+    share, x_far, og_far, valid, c_gain, s_gain, wq_far, wkv_far, wo_far, gate_far, up_far, down_far,
+    server_out, g_gate, g_up, g_down, normed_all, att_all, dqkv_all, cg_all, g_qkv_part, g_out_part,
+    x_own, og_own, wq, wkv, wo, gate_w, up_w, down_w,
+    q_all, kv_all, p_all,
+    cut_slots, rows_cot, rows_normed, hidden, d_gate, d_up,
     served, served_in, home_in, home_out, sums, result, give, give_in, passing, pass_in,
-    load_sem, store_sem, early_sems, late_sems, cut_sems, cot_sems,
+    load_sem, early_sems, late_sems, cut_sems, cot_sems,
     swap_sems, part_sems, home_sems, pass_sems, half_sems,
 ):
     members, groups = lax.axis_size("mem"), lax.axis_size("grp")
@@ -152,16 +160,12 @@
 
     loads = {}
     for i, (name, far, near) in enumerate((
-        ("wq", wq_far, wq), ("wkv", wkv_far, wkv), ("wo", wo_far, wo),
+        ("x", x_far, x_own), ("og", og_far, og_own), ("wq", wq_far, wq), ("wkv", wkv_far, wkv), ("wo", wo_far, wo),
         ("down", down_far, down_w), ("gate", gate_far, gate_w), ("up", up_far, up_w),
     )):
         loads[name] = pltpu.make_async_copy(far, near, load_sem.at[i])
         loads[name].start()
-    stores = []
-
-    def store(near, far):
-        stores.append(pltpu.make_async_copy(near, far, store_sem.at[len(stores)]))
-        stores[-1].start()
+    met = greet(("grp", "mem"))
 
     keep_at = pl.multiple_of(odd * half, half)
     give_at = pl.multiple_of((1 - odd) * half, half)
@@ -169,22 +173,27 @@
     def half_slot(index, low, count):
         return cg_all.at[index, pl.ds(pl.multiple_of(keep_at + low, 8), count)]
 
-    def whole(ref):
-        return lambda index, low, count: ref.at[index, pl.ds(low, count)]
+    def whole(ref, base=0):
+        return lambda index, low, count: ref.at[index, pl.ds(base + low, count)]
 
     cut = Gather("mem", whole(cut_slots), length, cut_sems)
-    cot = Gather("mem", whole(rows_cot), length, cot_sems)
+    cot_top = Gather("mem", whole(rows_cot), half, cot_sems[0])
+    cot_low = Gather("mem", whole(rows_cot, half), half, cot_sems[1])
     early = Gather("grp", whole(normed_all), length, early_sems, True)
     late = Gather("grp", half_slot, half, late_sems, True)
 
+    for name in ("x", "og"):
+        loads[name].wait()
     live = lax.broadcasted_iota(jnp.int32, (length, width), 0) < valid[0, 0]
     own_cot = jnp.where(live, og_own[...].astype(F32), 0.0)
     rows_cot[0] = own_cot.astype(BF16)
     sums[...] = own_cot
     x_float = x_own[...].astype(F32)
     normed_all[0] = (x_float * rms(x_float) * c_gain[...]).astype(BF16)
-    greet(("grp", "mem"))
-    cot.advance(0)
+    with jax.named_scope("greet"):
+        met()
+    cot_top.advance(0)
+    cot_low.advance(0, ring=False)
     early.advance(0)
 
     key_at = lax.broadcasted_iota(jnp.int32, (length, length), 0)
@@ -241,57 +250,93 @@
                 d_scores = d_scores.astype(BF16)
                 d_q = (dot(keys, d_scores) * SCALE).astype(BF16)
                 dqkv_all[pl.ds(kv * per_kv * HEAD_DIM, per_kv * HEAD_DIM), columns] = stacked(d_q)
-                dqkv_all[pl.ds(q_cols + kv * HEAD_DIM, HEAD_DIM), columns] = dot(
-                    q_all[slot, kv], d_scores, CONTRACT_LAST
+                both = dot(
+                    jnp.concatenate([q_all[slot, kv], d_cat], axis=0),
+                    jnp.concatenate([d_scores, probs], axis=0),
+                    CONTRACT_LAST,
                 ).astype(BF16)
-                dqkv_all[pl.ds(q_cols + kv_rows + kv * HEAD_DIM, HEAD_DIM), columns] = dot(
-                    d_cat, probs, CONTRACT_LAST
-                ).astype(BF16)
-
-    loads["wq"].wait()
-    loads["wkv"].wait()
-    forward(0, 1)
+                dqkv_all[pl.ds(q_cols + kv * HEAD_DIM, HEAD_DIM), columns] = both[:HEAD_DIM, :length]
+                dqkv_all[pl.ds(q_cols + kv_rows + kv * HEAD_DIM, HEAD_DIM), columns] = both[
+                    HEAD_DIM:, length:
+                ]
+
+    with jax.named_scope("wait_wq"):
+        loads["wq"].wait()
+        loads["wkv"].wait()
+    with jax.named_scope("forward_own"):
+        forward(0, 1)
     loads["wo"].wait()
     mixed = dot(att_all[:, pl.ds(0, length)], wo[...], CONTRACT_FIRST)
     cut_slots[0] = (x_own[...].astype(F32) + mixed).astype(BF16)
     cut.advance(0)
+    cot_low.pass_on(0)
 
     early_steps = list(range(1, group_pairs))
-    ready = [1, 1]
+    done = {"forward": 1, "backward": 0, "partial": 0}
 
     def keep_going():
         if early_steps:
             step = early_steps.pop(0)
-            early.advance(step)
-            ready[1] = 2 * step
+            with jax.named_scope(f"early_step{step}"):
+                early.advance(step)
 
     def recompute(limit):
-        while ready[0] < min(limit, groups):
-            first = ready[0]
+        while done["forward"] < min(limit, groups):
+            first = done["forward"]
             count = 1 if first % 2 else 2
-            early.take((first + count - 1) // 2)
-            forward(first, count)
-            ready[0] += count
+            step = (first + count - 1) // 2
+            while early_steps and early_steps[0] <= step:
+                keep_going()
+            with jax.named_scope(f"early_take{first}"):
+                early.take(step)
+            with jax.named_scope(f"forward{first}"):
+                forward(first, count)
+            done["forward"] += count
+
+    def weight_grad(left, right, near):
+        rows = right.shape[0] * length
+        near[...] = dot(left[...], right[...].reshape(rows, width), CONTRACT_FIRST).astype(BF16)
+
+    weight_grads = [
+        (hidden, rows_cot, g_down), (d_gate, rows_normed, g_gate), (d_up, rows_normed, g_up)
+    ]
+
+    def more():
+        if weight_grads:
+            with jax.named_scope(f"weight_grad{len(weight_grads)}"):
+                weight_grad(*weight_grads.pop(0))
+
+    def cot_hidden(p):
+        with jax.named_scope(f"wait_cot{p}"):
+            for part in (cot_top, cot_low):
+                if p > 1 or (p == 1 and part is cot_low):
+                    part.advance(p)
+            for part in (cot_top, cot_low):
+                part.take(p)
+        left = rows_cot[pl.ds(2 * p, 2)].reshape(2 * length, width)
+        return dot(left, down_w[...], CONTRACT_LAST)
 
     for p in range(pairs):
-        if p > 0:
-            cut.advance(p)
-            cot.advance(p)
-        cut.take(p)
-        cot.take(p)
         span = pl.ds(2 * p, 2)
+        if p == 0:
+            loads["down"].wait()
+            d_hidden = cot_hidden(0)
+        with jax.named_scope(f"wait_cut{p}"):
+            if p > 0:
+                cut.advance(p)
+            cut.take(p)
         h_float = cut_slots[span].reshape(2 * length, width).astype(F32)
         inv_rms = rms(h_float)
         normed = (h_float * inv_rms * s_gain[...]).astype(BF16)
         rows_normed[span] = normed.reshape(2, length, width)
         if p == 0:
-            for name in ("down", "gate", "up"):
+            for name in ("gate", "up"):
                 loads[name].wait()
-        d_hidden = dot(rows_cot[span].reshape(2 * length, width), down_w[...], CONTRACT_LAST)
         gate_act = dot(normed, gate_w[...], CONTRACT_LAST)
         up_act = dot(normed, up_w[...], CONTRACT_LAST)
         if p > 0:
-            keep_going()
+            d_hidden = cot_hidden(p)
+        keep_going()
         sigma = jax.nn.sigmoid(gate_act)
         acted = gate_act * sigma
         hidden_now = (acted * up_act).astype(BF16)
@@ -305,8 +350,10 @@
         pushed = norm_back(h_float, inv_rms, s_gain[...], d_normed)
         sums[...] += pushed[:length] + pushed[length:]
         served[span] = dot(hidden_now, down_w[...]).astype(BF16).reshape(2, length, width)
+        if p == 0 and pairs > 1:
+            with jax.named_scope("cot_step1"):
+                cot_top.advance(1)
         if p == 0:
-            keep_going()
             recompute(2)
 
     give[...] = sums[pl.ds(give_at, half)].astype(BF16)
@@ -316,7 +363,8 @@
     for p in range(pairs):
         swaps.append(send(served.at[2 * p + 1], served_in.at[p], swap_sems, p, partner))
         swaps[-1].start()
-    handed.wait_recv()
+    with jax.named_scope("wait_handed"):
+        handed.wait_recv()
     total = sums[pl.ds(keep_at, half)] + give_in[...].astype(F32)
     passing[...] = total.astype(BF16)
     passes = []
@@ -325,11 +373,12 @@
             send(passing, pass_in.at[k - 1], pass_sems, k - 1, {"mem": lax.rem(me + 2 * k, members)})
         )
         passes[-1].start()
+    recompute(4)
     keep_going()
-    recompute(4)
     homes = []
     for p in range(pairs):
-        swaps[p].wait_recv()
+        with jax.named_scope(f"wait_swap{p}"):
+            swaps[p].wait_recv()
         mine = served[2 * p].astype(F32) + served_in[p].astype(F32)
         if p == 0:
             result[...] = cut_slots[0].astype(F32) + mine
@@ -342,8 +391,10 @@
                 )
             )
             homes[-1].start()
+    more()
     for k in range(1, pairs):
-        passes[k - 1].wait_recv()
+        with jax.named_scope(f"wait_pass{k}"):
+            passes[k - 1].wait_recv()
         total = total + pass_in[k - 1].astype(F32)
     cg_all[0, pl.ds(keep_at, half)] = (total / members).astype(BF16)
 
@@ -354,69 +405,72 @@
         exchanged[slot] = send(ref, ref, half_sems, slot, partner)
         exchanged[slot].start()
 
+    def partial_grads(count):
+        some = pl.ds(0, count * length)
+        normed = normed_all[pl.ds(0, count)].reshape(count * length, width)
+        g_qkv_part[...] = dot(normed, dqkv_all[:, some], FIRST_WITH_LAST).astype(BF16)
+        upstream = cg_all[pl.ds(0, count)].reshape(count * length, width)
+        g_out_part[...] = dot(att_all[:, some], upstream).astype(BF16)
+
+    def pull(limit):
+        first = done["backward"]
+        while first < limit:
+            count = min(4, limit - first)
+            recompute(first + count)
+            for slot in range(first, first + count):
+                with jax.named_scope(f"wait_exchange{slot}"):
+                    exchanged[slot].wait_recv()
+            with jax.named_scope(f"backward{first}"):
+                backward(first, count)
+            first += count
+        done["backward"] = first
+
     late.advance(0)
     exchange(0)
-    keep_going()
-
-    def weight_grad(left, right, near, far):
-        rows = right.shape[0] * length
-        near[...] = dot(left[...], right[...].reshape(rows, width), CONTRACT_FIRST).astype(BF16)
-        store(near, far)
-
-    weight_grads = [
-        (hidden, rows_cot, g_down, g_down_far),
-        (d_gate, rows_normed, g_gate, g_gate_far),
-        (d_up, rows_normed, g_up, g_up_far),
-    ]
-
-    def more():
-        if weight_grads:
-            weight_grad(*weight_grads.pop(0))
-
     recompute(6)
     more()
-    while early_steps:
-        keep_going()
     for step in range(1, group_pairs):
-        late.advance(step)
+        with jax.named_scope(f"late_step{step}"):
+            late.advance(step)
         exchange(2 * step)
-        late.take(step - 1)
+        with jax.named_scope(f"late_take{step - 1}"):
+            late.take(step - 1)
         exchange(2 * step - 1)
-        recompute(groups if step > 1 else 6)
-        more()
         if step == 1:
+            recompute(8)
             for p in range(1, pairs):
-                homes[p - 1].wait_recv()
+                with jax.named_scope("wait_home"):
+                    homes[p - 1].wait_recv()
                 result[...] += home_in[p - 1].astype(F32)
-            served[0] = result[...].astype(BF16)
-            store(served.at[0], server_out_far)
-        if step > 1:
-            for slot in (2 * step - 4, 2 * step - 3):
-                exchanged[slot].wait_recv()
-            backward(2 * step - 4, 2)
+            server_out[...] = result[...].astype(BF16)
+        elif step % 2 == 0:
+            more()
+            pull(2 * step)
+        if step == group_pairs - 1 and done["backward"] >= share > 0:
+            with jax.named_scope("partial"):
+                partial_grads(share)
+            done["partial"] = share
     while early_steps:
         keep_going()
     recompute(groups)
     while weight_grads:
         more()
-    store(normed_all, normed_far)
-    store(att_all, att_far)
-    late.take(group_pairs - 1)
+    with jax.named_scope("late_last"):
+        late.take(group_pairs - 1)
     exchange(groups - 1)
-    for first in range(max(groups - 4, 0), groups, 2):
-        for slot in (first, first + 1):
-            exchanged[slot].wait_recv()
-        backward(first, 2)
-    store(cg_all, cg_far)
-    store(dqkv_all, dqkv_far)
+    pull(groups)
+    if not share:
+        g_qkv_part[...] = jnp.zeros_like(g_qkv_part)
+        g_out_part[...] = jnp.zeros_like(g_out_part)
+    elif not done["partial"]:
+        partial_grads(share)
     early.finish()
     late.finish()
     cut.finish()
-    cot.finish()
+    cot_top.finish()
+    cot_low.finish()
     for copy in [handed] + swaps + passes + homes + list(exchanged.values()):
         copy.wait_send()
-    for copy in stores:
-        copy.wait()
 
 
 def step_call(x, og, valid, c_gain, s_gain, wq, wkv, wo, gate_t, up_t, down):
@@ -429,39 +483,36 @@
     half = length // 2
     rows = members * length
     tokens = groups * length
-    shape = jax.ShapeDtypeStruct
+    kept = [
+        (length, width), (units, width), (units, width), (units, width), (groups, length, width),
+        (q_cols, tokens), (q_cols + kv_cols, tokens), (groups, length, width),
+        (width, q_cols + kv_cols), (q_cols, width),
+    ]
+    keep = 2 * sum(math.prod(dims) for dims in kept) < 20 * 2**20
+    share = groups // 2 if keep else 0
+    if not share:
+        kept[-2:] = [(16, 128)] * 2
+    shape = lambda *dims: pltpu.VMEM(dims, BF16) if keep else jax.ShapeDtypeStruct(dims, BF16)
     near = pl.BlockSpec(memory_space=pltpu.VMEM)
     far = pl.BlockSpec(memory_space=pl.ANY)
+    stay = lambda a: pltpu.with_memory_space_constraint(a, pltpu.HBM)
     others = max(pairs - 1, 1)
     two = lambda count: [pltpu.SemaphoreType.DMA((count,))] * 2
     vmem = lambda *dims: pltpu.VMEM(dims, BF16)
-    return pl.pallas_call(
-        step_kernel,
-        out_shape=[
-            shape((length, width), BF16),
-            shape((units, width), BF16),
-            shape((units, width), BF16),
-            shape((units, width), BF16),
-            shape((groups, length, width), BF16),
-            shape((q_cols, tokens), BF16),
-            shape((q_cols + kv_cols, tokens), BF16),
-            shape((groups, length, width), BF16),
-        ],
-        in_specs=[near] * 2 + [pl.BlockSpec(memory_space=pltpu.SMEM)] + [near] * 2 + [far] * 6,
-        out_specs=[far] * 8,
+    return share, pl.pallas_call(
+        functools.partial(step_kernel, share),
+        out_shape=[shape(*dims) for dims in kept],
+        in_specs=[far] * 2 + [pl.BlockSpec(memory_space=pltpu.SMEM)] + [near] * 2 + [far] * 6,
+        out_specs=[near] * 10,
         scratch_shapes=[
+            vmem(length, width), vmem(length, width),
             vmem(*wq.shape), vmem(*wkv.shape), vmem(*wo.shape),
             vmem(units, width), vmem(units, width), vmem(units, width),
-            vmem(groups, length, width),
             vmem(groups, KV_HEADS, HEAD_DIM, per_kv * length),
             vmem(groups, kv_cols, length),
             vmem(groups, KV_HEADS, length, per_kv * length),
-            vmem(q_cols, tokens),
-            vmem(q_cols + kv_cols, tokens),
-            vmem(groups, length, width),
             vmem(members, length, width), vmem(members, length, width), vmem(members, length, width),
             vmem(rows, units), vmem(rows, units), vmem(rows, units),
-            vmem(units, width), vmem(units, width), vmem(units, width),
             vmem(members, length, width),
             vmem(pairs, length, width),
             vmem(others, length, width),
@@ -470,34 +521,25 @@
             pltpu.VMEM((length, width), F32),
             vmem(half, width), vmem(half, width), vmem(half, width),
             vmem(others, half, width),
-            pltpu.SemaphoreType.DMA((6,)),
             pltpu.SemaphoreType.DMA((8,)),
-            gather_sems(groups), gather_sems(groups), gather_sems(members), gather_sems(members),
+            gather_sems(groups), gather_sems(groups), gather_sems(members), [gather_sems(members)] * 2,
             two(pairs), two(1), two(others), two(others), two(groups),
         ],
         compiler_params=pltpu.CompilerParams(
-            collective_id=0, has_side_effects=True, vmem_limit_bytes=67043328
+            collective_id=0, has_side_effects=True, vmem_limit_bytes=38 * 2**20 if keep else VMEM_MOST
         ),
         name="step",
-    )(x, og, valid, c_gain, s_gain, wq, wkv, wo, gate_t, up_t, down)
+    )(stay(x), stay(og), valid, *map(stay, (c_gain, s_gain, wq, wkv, wo, gate_t, up_t, down)))
 
 
 def grads_kernel(
-    groups, server_far, gate_far, up_far, down_far, normed_far, att_far, dqkv_far, cg_far,
+    share, groups, server, gate, up, down, normed, att, dqkv, cg, qkv_part, out_part,
     server_out, g_query_out, g_keyval_out, g_out_out, g_gate_out, g_up_out, g_down_out,
-    server, gate, up, down, normed, att, dqkv, cg, g_query, g_keyval, g_out, load_sem, store_sem,
+    g_query, g_keyval, g_out, store_sem,
 ):
     tokens = att.shape[1]
     width = normed.shape[2]
     columns = g_query.shape[1]
-    loads = {}
-    for i, (name, source, near) in enumerate((
-        ("att", att_far, att), ("cg", cg_far, cg), ("normed", normed_far, normed),
-        ("dqkv", dqkv_far, dqkv), ("down", down_far, down), ("gate", gate_far, gate),
-        ("up", up_far, up), ("server", server_far, server),
-    )):
-        loads[name] = pltpu.make_async_copy(source, near, load_sem.at[i])
-        loads[name].start()
     stores = []
 
     def store(near, out):
@@ -505,45 +547,47 @@
         stores[-1].start()
 
     scale = 1.0 / groups
-    loads["att"].wait()
-    loads["cg"].wait()
-    g_out[...] = (dot(att[...], cg[...].reshape(tokens, width)) * scale).astype(BF16)
-    store(g_out, g_out_out)
-    loads["normed"].wait()
-    loads["dqkv"].wait()
-    for name, near, out in (("down", down, g_down_out), ("gate", gate, g_gate_out)):
-        loads[name].wait()
+    for near, out in ((down, g_down_out), (gate, g_gate_out), (up, g_up_out), (server, server_out)):
         store(near, out)
-    grads = dot(normed[...].reshape(tokens, width), dqkv[...], FIRST_WITH_LAST) * scale
+    rest = groups - share
+    some = pl.ds(tokens - rest * (tokens // groups), rest * (tokens // groups))
+    left = normed[pl.ds(groups - rest, rest)].reshape(-1, width)
+    grads = dot(left, dqkv[:, some], FIRST_WITH_LAST)
+    if share:
+        grads = grads + qkv_part[...].astype(F32)
+    grads = grads * scale
     g_query[...] = grads[:, :columns].astype(BF16)
     store(g_query, g_query_out)
     g_keyval[...] = grads[:, columns:].astype(BF16)
     store(g_keyval, g_keyval_out)
-    for name, near, out in (("up", up, g_up_out), ("server", server, server_out)):
-        loads[name].wait()
-        store(near, out)
+    right = cg[pl.ds(groups - rest, rest)].reshape(-1, width)
+    grads = dot(att[:, some], right)
+    if share:
+        grads = grads + out_part[...].astype(F32)
+    g_out[...] = (grads * scale).astype(BF16)
+    store(g_out, g_out_out)
     for copy in stores:
         copy.wait()
 
 
-def grads_call(columns, *arrays):
-    server, gate, up, down, normed, att, dqkv, cg = arrays
+def grads_call(share, columns, *arrays):
+    server, gate, up, down, normed, att, dqkv, cg, qkv_part, out_part = arrays
     groups, _, width = normed.shape
     wide = dqkv.shape[0]
     far = pl.BlockSpec(memory_space=pl.ANY)
+    near = pl.BlockSpec(memory_space=pltpu.VMEM)
     outs = [
         server.shape, (width, columns), (width, wide - columns), (att.shape[0], width),
         gate.shape, up.shape, down.shape,
     ]
     return pl.pallas_call(
-        lambda *refs: grads_kernel(groups, *refs),
+        functools.partial(grads_kernel, share, groups),
         out_shape=[jax.ShapeDtypeStruct(o, BF16) for o in outs],
-        in_specs=[far] * len(arrays),
+        in_specs=[near if share else far] * 4 + [near] * 6,
         out_specs=[far] * len(outs),
-        scratch_shapes=[pltpu.VMEM(a.shape, BF16) for a in arrays]
-        + [pltpu.VMEM(o, BF16) for o in outs[1:4]]
-        + [pltpu.SemaphoreType.DMA((len(arrays),)), pltpu.SemaphoreType.DMA((len(outs),))],
-        compiler_params=pltpu.CompilerParams(vmem_limit_bytes=67043328),
+        scratch_shapes=[pltpu.VMEM(o, BF16) for o in outs[1:4]]
+        + [pltpu.SemaphoreType.DMA((len(outs),))],
+        compiler_params=pltpu.CompilerParams(vmem_limit_bytes=20 * 2**20 if share else VMEM_MOST),
         name="grads",
     )(*arrays)
 
@@ -561,12 +605,12 @@
     out_grad,
     valid,
 ):
-    server, gate, up, down, normed, att, dqkv, cg = step_call(
+    share, results = step_call(
         client_input[0, 0], out_grad[0, 0], valid, client_gain, server_gain,
         w_query[0], w_keyval[0], w_out[0], w_gate[0].T, w_up[0].T, w_down[0],
     )
     (server_out, grad_query, grad_keyval, grad_out, grad_gate, grad_up, grad_down) = grads_call(
-        w_query.shape[2], server, gate, up, down, normed, att, dqkv, cg
+        share, w_query.shape[2], *results
     )
     return (
         server_out[None, None],

time: 70.1 us -> 58.8 us (0.84)
  the two profiles are of different devices: /device:TPU:0 before, /device:TPU:1 now
where the time goes in v2:
time: 58.8 us; the launch traced here: 58.6 us
  Pallas kernels  57.1 us (97%)
  between operations  1.47 us (2%)
    pallas_call x1, Pallas kernels, step_call(): pl.pallas_call(functools.partial(step_kernel, share), out_shape=[shape(*d...  53.1 us
    pallas_call x1, Pallas kernels, grads_call(): pl.pallas_call(functools.partial(grads_kernel, share, groups), out_shape=...  4 us

profile of v2, /device:TPU:1, one launch (start us, length us, event | category | flops | bytes accessed | tf_op | source)
XLA Modules:
  0.0 58.6 jit_solution(13187644053068884716)
XLA Ops:
  1.3 53.1 %step.1 = (bf16[128,896]{1,0:T(8,128)(2,1)S(1)}, bf16[1216,896]{1,0:T(8,128)(2,1)S(1)}, bf16[1216,896]{1,0:T(8,128)(2,1)S(1)}, bf16[1216,896]{1,0:T(8,128)(2,1)S...) custom-call(bf16[128,896]{1,0:T(8,128)(2,1)} %bitcast.29, ...), custom_call_target="tpu_custom_call" | custom-call | tf_op jit(solution)/shard_map/step/pallas_call | solution.py:502
  54.4 4.0 %grads.1 = (bf16[128,896]{1,0:T(8,128)(2,1)}, bf16[896,896]{1,0:T(8,128)(2,1)}, bf16[896,256]{1,0:T(8,128)(2,1)}, bf16[896,896]{1,0:T(8,128)(2,1)}, bf16[1216,89...) custom-call(bf16[128,896]{1,0:T(8,128)(2,1)S(1)} %get-tuple-element.24.server, ...), custom_call_target="tpu_custom_call" | custom-call | tf_op jit(solution)/shard_map/grads/pallas_call | solution.py:583

commit v3 on v2

--- a/solution.py
+++ b/solution.py
@@ -180,7 +180,13 @@
     cot_top = Gather("mem", whole(rows_cot), half, cot_sems[0])
     cot_low = Gather("mem", whole(rows_cot, half), half, cot_sems[1])
     early = Gather("grp", whole(normed_all), length, early_sems, True)
-    late = Gather("grp", half_slot, half, late_sems, True)
+    quarter = half // 2
+    late_top = Gather("grp", half_slot, quarter, late_sems[0], True)
+    late_low = Gather(
+        "grp", lambda index, low, count: half_slot(index, quarter + low, count),
+        quarter, late_sems[1], True,
+    )
+    late = (late_top, late_low)
 
     for name in ("x", "og"):
         loads[name].wait()
@@ -425,16 +431,19 @@
             first += count
         done["backward"] = first
 
-    late.advance(0)
+    for part in late:
+        part.advance(0)
     exchange(0)
     recompute(6)
     more()
     for step in range(1, group_pairs):
         with jax.named_scope(f"late_step{step}"):
-            late.advance(step)
+            for part in late:
+                part.advance(step)
         exchange(2 * step)
         with jax.named_scope(f"late_take{step - 1}"):
-            late.take(step - 1)
+            for part in late:
+                part.take(step - 1)
         exchange(2 * step - 1)
         if step == 1:
             recompute(8)
@@ -456,7 +465,8 @@
     while weight_grads:
         more()
     with jax.named_scope("late_last"):
-        late.take(group_pairs - 1)
+        for part in late:
+            part.take(group_pairs - 1)
     exchange(groups - 1)
     pull(groups)
     if not share:
@@ -465,7 +475,8 @@
     elif not done["partial"]:
         partial_grads(share)
     early.finish()
-    late.finish()
+    for part in late:
+        part.finish()
     cut.finish()
     cot_top.finish()
     cot_low.finish()
@@ -522,7 +533,7 @@
             vmem(half, width), vmem(half, width), vmem(half, width),
             vmem(others, half, width),
             pltpu.SemaphoreType.DMA((8,)),
-            gather_sems(groups), gather_sems(groups), gather_sems(members), [gather_sems(members)] * 2,
+            gather_sems(groups), [gather_sems(groups)] * 2, gather_sems(members), [gather_sems(members)] * 2,
             two(pairs), two(1), two(others), two(others), two(groups),
         ],
         compiler_params=pltpu.CompilerParams(

time: 58.8 us -> 58.3 us (level)
  no operation moved by 1% of the time
where the time goes in v3:
time: 58.3 us; the launch traced here: 58.1 us
  Pallas kernels  56.7 us (97%)
  between operations  1.47 us (3%)
    pallas_call x1, Pallas kernels, step_call(): pl.pallas_call(functools.partial(step_kernel, share), out_shape=[shape(*d...  52.7 us
    pallas_call x1, Pallas kernels, grads_call(): pl.pallas_call(functools.partial(grads_kernel, share, groups), out_shape=...  4 us

profile of v3, /device:TPU:1, one launch (start us, length us, event | category | flops | bytes accessed | tf_op | source)
XLA Modules:
  0.0 58.1 jit_solution(10949216412566109017)
XLA Ops:
  1.3 52.7 %step.1 = (bf16[128,896]{1,0:T(8,128)(2,1)S(1)}, bf16[1216,896]{1,0:T(8,128)(2,1)S(1)}, bf16[1216,896]{1,0:T(8,128)(2,1)S(1)}, bf16[1216,896]{1,0:T(8,128)(2,1)S...) custom-call(bf16[128,896]{1,0:T(8,128)(2,1)} %bitcast.29, ...), custom_call_target="tpu_custom_call" | custom-call | tf_op jit(solution)/shard_map/step/pallas_call | solution.py:513
  54.0 4.0 %grads.1 = (bf16[128,896]{1,0:T(8,128)(2,1)}, bf16[896,896]{1,0:T(8,128)(2,1)}, bf16[896,256]{1,0:T(8,128)(2,1)}, bf16[896,896]{1,0:T(8,128)(2,1)}, bf16[1216,89...) custom-call(bf16[128,896]{1,0:T(8,128)(2,1)S(1)} %get-tuple-element.24.server, ...), custom_call_target="tpu_custom_call" | custom-call | tf_op jit(solution)/shard_map/grads/pallas_call | solution.py:594
